TPU v7x, 32 devices: a whole 2x2x4 slice. The times are simulated.
32 devices in a mesh: parts: 2 (over x), rows: 16 (over z, y, core).
Axes of the slice: x: 2, y: 2, z: 4, core: 2. Of those that a mesh axis runs over, the one named last changes fastest.
Arguments:
- feature_bin: int32 [16384, 700], P(('parts', 'rows')), parts along dimension 0, may hold values from 0 to 255
- doc_leaf: int32 [16384], P(('parts', 'rows')), parts along dimension 0, may hold values from 0 to 31
- current_score: float32 [16384], P(('parts', 'rows')), parts along dimension 0, may hold values from -8 to 8
- relevance: int32 [16384], P(('parts', 'rows')), parts along dimension 0, may hold values from 0 to 4
- doc_rank: int32 [16384], P(('parts', 'rows')), parts along dimension 0, may hold values from 0 to 255, as said below
- query_length: int32 [64], P(('parts', 'rows')), parts along dimension 0, may hold values from 10 to 256, as said below
- feature_votes: int32 [32, 32, 20], P(('parts', 'rows')), parts along dimension 0, may hold values from 0 to 699, all different within a row
- elected: int32 [64, 40], P('parts'), parts along dimension 0, may hold values from 0 to 699, all different within a row
Outputs:
- gradient: float32 [16384], P(('parts', 'rows')), parts along dimension 0
- hessian: float32 [16384], P(('parts', 'rows')), parts along dimension 0
- vote_count: int32 [64, 700], P('parts'), parts along dimension 0
- split_gain: float32 [64, 40, 256], P('parts'), parts along dimension 0
There are 2 independent parts, one for each index of `parts`. A program takes and returns all parts, laid end to end along the dimension named above; each array names one. Nothing has to cross between parts.
Inputs may be any that keep to these rules, and one draw needn't show every extreme that they name: `query_length`: query q holds slots q * 256 to (q + 1) * 256 - 1 of the document arrays; in every draw some query has exactly 256 documents. `doc_rank`: within each query the live documents hold positions 0 to query_length - 1, each once; slots that are not live hold positions from query_length to 255. `feature_votes`: the 20 votes of one device for one leaf are different features. The 40 elected features of one leaf are different.
All inputs are finite; a program needn't handle non-finite values.
Results may differ from a plain program's by a relative error of at most 0.0003.
Values sent between devices are 32-bit elements; how exact they have to be, the bound alone decides.
No kernel may reach another device: no remote copies, remote signals or barrier semaphores. Data moves between devices by JAX's collectives and lax.ppermute only.
A program may use at most 64 MiB of HBM per device.

v0:
```python
import math
import jax
import jax.numpy as jnp
from jax import lax
from jax.sharding import PartitionSpec as P

B = 256
QMAX = 256
ridge_weight = 1.0


def query_terms(scores, levels, places, length):
    positions = jnp.arange(scores.shape[0], dtype=jnp.int32)
    living = positions < length
    gains = jnp.exp2(levels.astype(jnp.float32)) - 1.0
    discount = 1.0 / jnp.log2(places.astype(jnp.float32) + 2.0)
    higher = (levels[None, :] > levels[:, None]) & living[None, :]
    earlier = (
        (levels[None, :] == levels[:, None])
        & (positions[None, :] < positions[:, None])
        & living[None, :]
    )
    ideal_place = jnp.sum((higher | earlier).astype(jnp.float32), axis=1)
    ideal = jnp.sum(jnp.where(living, gains / jnp.log2(ideal_place + 2.0), 0.0))
    scaling = 1.0 / jnp.maximum(ideal, 1.0)
    ordered = (levels[:, None] > levels[None, :]) & living[:, None] & living[None, :]
    chance = jax.nn.sigmoid(scores[None, :] - scores[:, None])
    change = (
        (gains[:, None] - gains[None, :]) * jnp.abs(discount[:, None] - discount[None, :]) * scaling
    )
    pushes = jnp.where(ordered, chance * change, 0.0)
    curves = jnp.where(ordered, chance * (1.0 - chance) * change, 0.0)
    return (
        jnp.sum(pushes, axis=0) - jnp.sum(pushes, axis=1),
        jnp.sum(curves, axis=0) + jnp.sum(curves, axis=1),
    )


def build_histogram(feature_bin, doc_leaf, gradient, hessian, elected, bins):
    leaves, picked = elected.shape
    documents = feature_bin.shape[0]
    leaf_hot = (doc_leaf[:, None] == jnp.arange(leaves, dtype=jnp.int32)[None, :]).astype(
        jnp.float32
    )
    columns = jnp.dot(
        leaf_hot, elected.astype(jnp.float32), precision=lax.Precision.HIGHEST
    ).astype(jnp.int32)
    chosen = jnp.take_along_axis(feature_bin, columns, axis=1)
    weighted = jnp.concatenate([leaf_hot * gradient[:, None], leaf_hot * hessian[:, None]], axis=1)
    block_rows = math.gcd(documents, 512)
    block_count = documents // block_rows
    bin_ids = jnp.arange(bins, dtype=jnp.int32)

    def add_block(index, total):
        onehot = (chosen[:, :, None] == bin_ids[None, None, :]).astype(jnp.float32)
        onehot = onehot.reshape(block_rows, picked * bins)
        return total + jnp.dot(weighted.T, onehot, precision=lax.Precision.HIGHEST)

    empty = jnp.zeros((2 * leaves, picked * bins), jnp.float32)
    total = lax.fori_loop(0, block_count, add_block, empty)
    return total.reshape(2, leaves, picked, bins)


def split_score(prefix, whole):
    remain = whole - prefix
    return (
        prefix[0] * prefix[0] / (prefix[1] + ridge_weight)
        + remain[0] * remain[0] / (remain[1] + ridge_weight)
        - whole[0] * whole[0] / (whole[1] + ridge_weight)
    )


def count_votes(feature_votes, features):
    hits = feature_votes[..., None] == jnp.arange(features, dtype=jnp.int32)
    return jnp.sum(hits.astype(jnp.int32), axis=(0, 2))


def on_device(
    feature_bin, doc_leaf, current_score, relevance, doc_rank, query_length, feature_votes, elected
):
    features = feature_bin.shape[1]
    all_votes = lax.all_gather(feature_votes, "rows", axis=0, tiled=True)
    vote_count = count_votes(all_votes, features)

    def one_query(items):
        return query_terms(items[0], items[1], items[2], items[3])

    gradient, hessian = lax.map(
        one_query,
        (
            current_score.reshape(-1, QMAX),
            relevance.reshape(-1, QMAX),
            doc_rank.reshape(-1, QMAX),
            query_length,
        ),
    )
    gradient = gradient.reshape(-1)
    hessian = hessian.reshape(-1)
    histogram = build_histogram(feature_bin, doc_leaf, gradient, hessian, elected, B)
    summed = lax.psum(histogram, "rows")
    prefix = jnp.cumsum(summed, axis=3)
    whole = jnp.sum(summed, axis=3, keepdims=True)
    split_gain = split_score(prefix, whole)
    return (gradient, hessian, vote_count, split_gain)


def solution(mesh):
    return jax.shard_map(
        on_device,
        mesh=mesh,
        in_specs=(
            P(("parts", "rows"), None),
            P(("parts", "rows")),
            P(("parts", "rows")),
            P(("parts", "rows")),
            P(("parts", "rows")),
            P(("parts", "rows")),
            P(("parts", "rows"), None, None),
            P("parts", None),
        ),
        out_specs=(
            P(("parts", "rows")),
            P(("parts", "rows")),
            P("parts", None),
            P("parts", None, None),
        ),
        check_vma=False,
    )
```

profile of v0, /device:TPU:0, one launch (start us, length us, event | category | flops | bytes accessed | tf_op | source)
XLA Modules:
  0.0 409.0 jit_solution(16073954382203800596)
XLA Ops:
  7.3 0.8 reshape.169
  8.0 0.7 reshape.170
  8.7 0.7 reshape.171
  9.4 9.2 %while.18 = (s32[]{:T(128)}, f32[2,256]{1,0:T(2,128)S(1)}, f32[2,256]{1,0:T(2,128)S(1)}, s32[2,256]{1,0:T(2,128)S(1)}, s32[2]{0:T(128)}, /*index=5*/f32[2,256]{1...) while((s32[]{:T(128)}, f32[2,256]{1,0:T(2,128)S(1)}, f32[2,256]{1,0:T(2,128)S(1)}, ...), condition=%wide.region_7.8_spmd, body=%wide.region_0.7_spmd.sunk | while | flops 2035203 | bytes 32681 | solution.py:88
  9.5 1.2 dynamic_slice.34
  10.7 0.6 iota_compare_fusion.6
  11.6 1.3 exponential_add_fusion.5
  13.5 0.4 fusion.28
  14.1 1.2 dynamic_slice.34
  15.3 0.6 iota_compare_fusion.6
  16.0 0.2 convert_reduce_fusion.3
  16.2 1.3 exponential_add_fusion.5
  18.2 0.4 fusion.28
  18.7 1.0 bitcast_or_fusion
  20.0 163.1 %gather_fusion = s32[20480]{0:T(1024)S(1)} fusion(s32[512,700]{0,1:T(8,128)S(1)} %copy-done, s32[20480]{0:T(1024)S(1)} %reshape.179), kind=kCustom, calls=%fused_computation | custom fusion | bytes 327680 | tf_op jit(solution)/shard_map/jit(take_along_axis)/gather | solution.py:48
  183.5 3.3 bitcast_compare_fusion
  186.8 11.0 %fusion.22 = f32[2,32,40,256]{3,1,2,0:T(8,128)} fusion(f32[2,32,512,1]{2,1,3,0:T(8,128)S(1)} %bitcast.69, pred[40,256,512,1]{2,1,0,3:T(32,128)(4,1)S(1)} %bitcast.68), kind=kOutput, calls=%fused_computation.56 | convolution fusion | flops 4026531840 | bytes 7995392 | tf_op jit(solution)/shard_map/while/body/eval_jaxpr/dot_general | solution.py:57
  197.9 0.7 copy-done.2
  198.6 24.5 %all_gather.3 = s32[16,32,20]{1,2,0:T(8,128)S(1)} all-gather(s32[1,32,20]{1,2,0:T(8,128)S(1)} %copy.33), channel_id=1, replica_groups=mesh['parts'=2,'rows'=16] {'rows'}, dimensions={0}, use_global_device_ids=true | all-gather | bytes 43520 | tf_op jit(solution)/shard_map/all_gather | solution.py:82
  223.1 4.4 %convert_reduce_fusion.1 = s32[32,700]{1,0:T(8,128)} fusion(s32[16,32,20]{1,2,0:T(8,128)S(1)} %all_gather.3), kind=kLoop, calls=%fused_computation.25 | loop fusion | flops 21481600 | bytes 130560 | tf_op jit(solution)/shard_map/reduce_sum | solution.py:75
  227.5 74.4 %all-reduce.2.cloned.1.call-done = f32[2,32,40,256]{3,1,2,0:T(8,128)} async-done(((f32[2,32,40,256]{3,1,2,0:T(8,128)}), f32[2,32,40,256]{3,1,2,0:T(8,128)}) %all-reduce.2.cloned.1.call-update) | async-done | bytes 2621456 | tf_op jit(solution)/shard_map/psum | solution.py:100
  302.0 2.2 reduce_sum.91
  304.2 4.3 %reshape.175 = f32[2,32,40,2,128]{4,3,1,2,0:T(2,128)} reshape(f32[2,32,40,256]{3,1,2,0:T(8,128)} %all-reduce.2.cloned.1.call-done) | data formatting | bytes 5242880 | tf_op jit(solution)/shard_map/reshape.2
  308.5 4.8 %copy.36 = f32[2,32,40,2,128]{4,2,3,1,0:T(8,128)} copy(f32[2,32,40,2,128]{4,3,1,2,0:T(2,128)} %reshape.175) | data formatting | bytes 5242880 | tf_op jit(solution)/shard_map/reshape.2
  313.3 69.9 %reduce-window.6 = f32[2,32,40,2,128]{4,2,3,1,0:T(8,128)} reduce-window(f32[2,32,40,2,128]{4,2,3,1,0:T(8,128)} %copy.36, f32[]{:T(128)} %constant.79.clone.1), window={size=1x1x1x1x128 pad=0_0x0_0x0_0x0_0x127_0}, to_apply=%region_10.11 | reduce-window | flops 83230720 | bytes 5242884 | tf_op jit(solution)/shard_map/reduce-window
  383.1 4.0 slice.41
  387.1 2.7 copy.37
  390.0 2.3 broadcast_add_fusion
  392.5 2.3 bitcast_subtract_fusion
  395.0 1.7 copy.39
  396.7 2.3 div.58
  399.1 3.1 fusion.12
  (47 shorter events, 1.9 us)
Async XLA Ops:
  7.2 12.8 %copy-start = (s32[512,700]{0,1:T(8,128)S(1)}, s32[512,700]{0,1:T(8,128)}, u32[]{:S(2)}) copy-start(s32[512,700]{0,1:T(8,128)} %param.10) | copy-start | bytes 4300804
  7.2 294.8 %all-reduce.2.cloned.1.call-start = ((), (), s32[]{:S(2)}) async-start(), calls=%async_computation | async-start | bytes 5242880 | tf_op jit(solution)/shard_map/psum | solution.py:100
  18.6 164.8 %copy-start.3 = (f32[1,2,2,128]{3,1,2,0:T(2,128)}, f32[1,2,2,128]{3,1,2,0:T(2,128)S(1)}, u32[]{:S(2)}) copy-start(f32[1,2,2,128]{3,1,2,0:T(2,128)S(1)} %copy.45) | copy-start | bytes 6148
  18.7 164.8 %copy-start.4 = (f32[1,2,2,128]{3,1,2,0:T(2,128)}, f32[1,2,2,128]{3,1,2,0:T(2,128)S(1)}, u32[]{:S(2)}) copy-start(f32[1,2,2,128]{3,1,2,0:T(2,128)S(1)} %copy.46) | copy-start | bytes 6148
  20.0 163.4 %copy-start.5 = (s32[512]{0:T(512)S(1)}, s32[512]{0:T(512)}, u32[]{:S(2)}) copy-start(s32[512]{0:T(512)} %param.11) | copy-start | bytes 6148
  197.9 0.7 copy-start.2
  390.0 2.5 copy-start.1
Sparse Core Ops, SparseCore 0:
  198.0 103.8 all-reduce.1
where the time goes:
time: 417 us; the launch traced here: 409 us
  local copies, waits for them, and re-layouts  189 us (45%)
  other arithmetic  92.9 us (22%)
  waiting for transfers between devices  74.4 us (18%)
  blocking collectives  24.5 us (6%)
  between operations  14.3 us (3%)
  matrix products  12 us (3%)
    gather x5, local copies, waits for them, and re-layouts, build_histogram(): chosen = jnp.take_along_axis(feature_bin, columns, axis=1)  164 us
    psum x1, waiting for transfers between devices, on_device(): summed = lax.psum(histogram, 'rows')  74.4 us
    another operation x5, other arithmetic  72.3 us
    all_gather x1, blocking collectives, on_device(): all_votes = lax.all_gather(feature_votes, 'rows', axis=0, tiled=True)  24.5 us
    dot_general x1, matrix products, add_block(): return total + jnp.dot(weighted.T, onehot, precision=lax.Precision.HIGHEST)  11 us
    another operation x4, local copies, waits for them, and re-layouts  9.1 us
  transfers between devices with their start and end apart: 1, of which 1 were waited for; matrix products, arithmetic and copies ran while one was open for 1% of the time, Pallas kernels for 0%

commit v1 on v0

--- a/solution.py
+++ b/solution.py
@@ -97,7 +97,7 @@
     gradient = gradient.reshape(-1)
     hessian = hessian.reshape(-1)
     histogram = build_histogram(feature_bin, doc_leaf, gradient, hessian, elected, B)
-    summed = lax.psum(histogram, "rows")
+    summed = jnp.sum(jax.lax.all_gather(histogram, "rows"), axis=0)
     prefix = jnp.cumsum(summed, axis=3)
     whole = jnp.sum(summed, axis=3, keepdims=True)
     split_gain = split_score(prefix, whole)

time: 417 us -> 554 us (1.33)
  waiting for transfers between devices: 74.4 us -> 181 us
  other arithmetic: 92.9 us -> 127 us
    all_gather x0 -> x1, waiting for transfers between devices: none -> 181 us  [on_device(): summed = jnp.sum(jax.lax.all_gather(histogram, 'rows'), axis=0)]
    psum x1 -> x0, waiting for transfers between devices: 74.4 us -> none  [on_device(): summed = lax.psum(histogram, 'rows')]
    reduce_sum x0 -> x1, other arithmetic: none -> 16.6 us  [on_device(): summed = jnp.sum(jax.lax.all_gather(histogram, 'rows'), axis=0)]
    reduce_sum x1 -> x2, other arithmetic: 2.15 us -> 16.9 us  [on_device(): whole = jnp.sum(summed, axis=3, keepdims=True)]
    another operation x4 -> x3, local copies, waits for them, and re-layouts: 9.1 us -> 3.54 us
where the time goes in v1:
time: 554 us; the launch traced here: 546 us
  local copies, waits for them, and re-layouts  187 us (34%)
  waiting for transfers between devices  181 us (33%)
  other arithmetic  127 us (23%)
  blocking collectives  24.8 us (4%)
  between operations  14.3 us (3%)
  matrix products  10.5 us (2%)
    all_gather x1, waiting for transfers between devices, on_device(): summed = jnp.sum(jax.lax.all_gather(histogram, 'rows'), axis=0)  181 us
    gather x5, local copies, waits for them, and re-layouts, build_histogram(): chosen = jnp.take_along_axis(feature_bin, columns, axis=1)  164 us
    another operation x5, other arithmetic  71.9 us
    all_gather x1, blocking collectives, on_device(): all_votes = lax.all_gather(feature_votes, 'rows', axis=0, tiled=True)  24.8 us
    reduce_sum x2, other arithmetic, on_device(): whole = jnp.sum(summed, axis=3, keepdims=True)  16.9 us
    reduce_sum x1, other arithmetic, on_device(): summed = jnp.sum(jax.lax.all_gather(histogram, 'rows'), axis=0)  16.6 us
  transfers between devices with their start and end apart: 1, of which 1 were waited for; matrix products, arithmetic and copies ran while one was open for 1% of the time, Pallas kernels for 0%

profile of v1, /device:TPU:0, one launch (start us, length us, event | category | flops | bytes accessed | tf_op | source)
XLA Modules:
  0.0 546.1 jit_solution(1254323526472708985)
XLA Ops:
  7.3 0.8 reshape.174
  8.1 0.7 reshape.173
  8.7 0.7 reshape.175
  9.4 9.2 %while.18 = (s32[]{:T(128)}, f32[2,256]{1,0:T(2,128)S(1)}, f32[2,256]{1,0:T(2,128)S(1)}, s32[2,256]{1,0:T(2,128)S(1)}, s32[2]{0:T(128)}, /*index=5*/f32[2,256]{1...) while((s32[]{:T(128)}, f32[2,256]{1,0:T(2,128)S(1)}, f32[2,256]{1,0:T(2,128)S(1)}, ...), condition=%wide.region_7.8_spmd, body=%wide.region_0.7_spmd.sunk | while | flops 2035203 | bytes 32689 | solution.py:88
  9.4 1.2 dynamic_slice.34
  10.7 0.6 iota_compare_fusion.6
  11.6 1.3 exponential_add_fusion.5
  14.0 1.2 dynamic_slice.34
  15.3 0.6 iota_compare_fusion.6
  16.2 1.3 exponential_add_fusion.5
  18.2 0.4 fusion.28
  18.7 1.0 bitcast_or_fusion
  20.1 163.1 %gather_fusion = s32[20480]{0:T(1024)S(1)} fusion(s32[512,700]{0,1:T(8,128)S(1)} %copy-done, s32[20480]{0:T(1024)S(1)} %reshape.184), kind=kCustom, calls=%fused_computation | custom fusion | bytes 327680 | tf_op jit(solution)/shard_map/jit(take_along_axis)/gather | solution.py:48
  183.5 3.3 bitcast_compare_fusion
  186.8 9.5 %fusion.21 = f32[2,32,40,256]{3,1,2,0:T(8,128)S(1)} fusion(f32[2,32,512,1]{2,1,3,0:T(8,128)S(1)} %bitcast.77, pred[40,256,512,1]{2,1,0,3:T(32,128)(4,1)S(1)} %bitcast.75), kind=kOutput, calls=%fused_computation.55 | convolution fusion | flops 4026531840 | bytes 7995392 | tf_op jit(solution)/shard_map/while/body/eval_jaxpr/dot_general | solution.py:57
  196.3 3.0 copy.52
  199.4 0.7 copy-done.3
  200.1 24.8 %all_gather.6 = s32[16,32,20]{1,2,0:T(8,128)S(1)} all-gather(s32[1,32,20]{1,2,0:T(8,128)S(1)} %copy.49), channel_id=1, replica_groups=mesh['parts'=2,'rows'=16] {'rows'}, dimensions={0}, use_global_device_ids=true | all-gather | bytes 43520 | tf_op jit(solution)/shard_map/all_gather | solution.py:82
  224.9 4.4 convert_reduce_fusion.1
  229.3 181.2 %all-gather.3.cloned.1.call-done = f32[32,32,40,256]{3,2,1,0:T(8,128)} async-done(((f32[2,32,40,256]{3,2,1,0:T(8,128)}), f32[32,32,40,256]{3,2,1,0:T(8,128)}) %all-gather.3.cloned.1.call-update) | async-done | bytes 41943056 | tf_op jit(solution)/shard_map/all_gather | solution.py:100
  410.5 16.6 %reduce_sum.100 = f32[2,32,40,256]{3,2,1,0:T(8,128)} reduce(f32[16,2,32,40,256]{4,3,2,1,0:T(8,128)} %bitcast.74, f32[]{:T(128)} %constant.79.clone.1), dimensions={0}, to_apply=%region_9.10 | reduce | flops 9830400 | bytes 44564484 | tf_op jit(solution)/shard_map/reduce_sum | solution.py:100
  427.1 3.5 copy_bitcast_fusion
  430.6 69.8 %reduce-window.6 = f32[2,32,40,2,128]{4,2,3,1,0:T(8,128)} reduce-window(f32[2,32,40,2,128]{4,2,3,1,0:T(8,128)} %copy_bitcast_fusion, f32[]{:T(128)} %constant.79.clone.1), window={size=1x1x1x1x128 pad=0_0x0_0x0_0x0_0x127_0}, to_apply=%region_10.11 | reduce-window | flops 83230720 | bytes 5242884 | tf_op jit(solution)/shard_map/reduce-window
  500.4 16.9 %reduce.1 = f32[32,32,40]{2,1,0:T(8,128)S(1)} reduce(f32[32,32,40,256]{3,2,1,0:T(8,128)} %all-gather.3.cloned.1.call-done, f32[]{:T(128)} %constant.79.clone.1), dimensions={3}, to_apply=%region_12.13 | reduce | flops 10444800 | bytes 42106884 | tf_op jit(solution)/shard_map/reduce_sum | solution.py:102
  517.3 4.0 slice.41
  521.3 2.7 copy.56
  524.2 3.7 bitcast_subtract_fusion
  528.0 1.9 broadcast_add_fusion
  530.1 1.9 fusion.13
  532.0 1.7 copy.58
  533.8 2.4 div.58
  536.2 3.0 fusion.12
  (53 shorter events, 2.3 us)
Async XLA Ops:
  7.2 12.9 %copy-start = (s32[512,700]{0,1:T(8,128)S(1)}, s32[512,700]{0,1:T(8,128)}, u32[]{:S(2)}) copy-start(s32[512,700]{0,1:T(8,128)} %param.10) | copy-start | bytes 4300804
  7.2 403.4 %all-gather.3.cloned.1.call-start = ((), (), s32[]{:S(2)}) async-start(), calls=%async_computation | async-start | bytes 44564480 | tf_op jit(solution)/shard_map/all_gather | solution.py:100
  18.6 164.8 %copy-start.4 = (f32[1,2,2,128]{3,1,2,0:T(2,128)}, f32[1,2,2,128]{3,1,2,0:T(2,128)S(1)}, u32[]{:S(2)}) copy-start(f32[1,2,2,128]{3,1,2,0:T(2,128)S(1)} %copy.77) | copy-start | bytes 6148
  18.7 164.8 %copy-start.5 = (f32[1,2,2,128]{3,1,2,0:T(2,128)}, f32[1,2,2,128]{3,1,2,0:T(2,128)S(1)}, u32[]{:S(2)}) copy-start(f32[1,2,2,128]{3,1,2,0:T(2,128)S(1)} %copy.76) | copy-start | bytes 6148
  20.0 163.4 %copy-start.6 = (s32[512]{0:T(512)S(1)}, s32[512]{0:T(512)}, u32[]{:S(2)}) copy-start(s32[512]{0:T(512)} %param.11) | copy-start | bytes 6148
  199.4 0.7 copy-start.3
  524.2 3.7 copy-start.2
  533.8 5.5 %copy-start.1 = (s32[512,700]{0,1:T(8,128)S(1)}, s32[512,700]{0,1:T(8,128)}, u32[]{:S(2)}) copy-start(s32[512,700]{0,1:T(8,128)} %param.10) | copy-start | bytes 4300804
Sparse Core Ops, SparseCore 0:
  199.5 210.9 all-gather.2
